TPU v7x, 32 devices: a whole 2x2x4 slice. The times are simulated.
32 devices in a mesh: groups: 2 (over y), pages: 4 (over z), patches: 4 (over x, core).
Axes of the slice: x: 2, y: 2, z: 4, core: 2. Of those that a mesh axis runs over, the one named last changes fastest.
Arguments:
- queries: bfloat16 [16, 32, 128], P(('groups', 'pages'), 'patches'), parts along dimension 0, may hold values from -6 to 6
- gallery: bfloat16 [640, 1024, 128], P(('groups', 'pages'), 'patches'), parts along dimension 0, may hold values from -0.5 to 0.5
- page_rows: int32 [640], P('groups'), parts along dimension 0, may hold values from 0 to 319, as said below
- candidates: int32 [16, 32], P(('groups', 'pages')), parts along dimension 0, may hold values from 0 to 319, as said below
Outputs:
- scores: float32 [16, 32], P(('groups', 'pages')), parts along dimension 0
There are 2 independent parts, one for each index of `groups`. A program takes and returns all parts, laid end to end along the dimension named above; each array names one. Nothing has to cross between parts.
Inputs may be any that keep to these rules, and one draw needn't show every extreme that they name: A permutation: page id c is stored at row page_rows[c] of gallery, which lies on pages index page_rows[c] // 80. Each query's 32 page ids are distinct. The 2 queries of one pages index have at most 48 candidates stored on one pages index, and in every draw some pages index stores exactly 48 candidates of the queries of every pages index.
All inputs are finite; a program needn't handle non-finite values.
Results may differ from a plain program's by a relative error of at most 0.0003.
Values may be sent and summed in bfloat16 or wider, within the bound.
A program may use at most 64 MiB of HBM per device.

v0:
```python
import jax
import jax.numpy as jnp
from jax import lax
from jax.sharding import PartitionSpec as P

QT = 32
CAP = 48


def token_maxima(query_rows, gallery):
    page_count = gallery.shape[0]
    grouped = gallery.reshape(page_count // 8, 8, gallery.shape[1], gallery.shape[2])

    def per_block(block):
        sims = jnp.einsum("rd,bpd->brp", query_rows, block, preferred_element_type=jnp.float32)
        return jnp.max(sims, axis=2)

    result = lax.map(per_block, grouped)
    return result.reshape(page_count, query_rows.shape[0])


def slot_plan(storage, page_count, owner_count, query_count):
    flat_rows = storage.reshape(-1)
    holder = flat_rows // page_count
    local_page = flat_rows % page_count
    onehot = (holder[:, None] == jnp.arange(owner_count, dtype=jnp.int32)[None, :]).astype(
        jnp.int32
    )
    running = jnp.cumsum(onehot, axis=0) - onehot
    rank = jnp.sum(running * onehot, axis=1)
    query_ids = (
        lax.axis_index("pages") * query_count + jnp.arange(query_count, dtype=jnp.int32)[:, None]
    )
    query_ids = jnp.broadcast_to(query_ids, storage.shape).reshape(-1)
    codes = (
        jnp.full((owner_count, CAP), -1, jnp.int32)
        .at[holder, rank]
        .set(query_ids * page_count + local_page)
    )
    return (holder, rank, codes)


def body(queries, gallery, page_rows, candidates):
    query_count = queries.shape[0]
    page_count = gallery.shape[0]
    owner_count = lax.axis_size("pages")
    storage = jnp.take(page_rows, candidates, axis=0)
    local_tokens = lax.all_gather(queries, "patches", axis=1, tiled=True)
    shard_rows = lax.all_gather(local_tokens, "pages", axis=0, tiled=True)
    maxima = token_maxima(shard_rows.reshape(-1, shard_rows.shape[2]), gallery)
    part_count = lax.axis_size("patches")
    arrived = lax.all_to_all(maxima, "patches", split_axis=0, concat_axis=0, tiled=True)
    share_max = jnp.max(arrived.reshape(part_count, page_count // part_count, -1), axis=0)
    share_scores = jnp.mean(share_max.reshape(page_count // part_count, -1, QT), axis=2)
    page_scores = lax.all_gather(share_scores, "patches", axis=0, tiled=True)
    holder, rank, codes = slot_plan(storage, page_count, owner_count, query_count)
    incoming = lax.all_to_all(codes, "pages", split_axis=0, concat_axis=0, tiled=True)
    safe_codes = jnp.maximum(incoming, 0)
    picked = page_scores[safe_codes % page_count, safe_codes // page_count]
    picked = jnp.where(incoming >= 0, picked, 0.0)
    returned = lax.all_to_all(picked, "pages", split_axis=0, concat_axis=0, tiled=True)
    return returned[holder, rank].reshape(storage.shape)


def solution(mesh):
    in_specs = (
        P(("groups", "pages"), "patches", None),
        P(("groups", "pages"), "patches", None),
        P("groups"),
        P(("groups", "pages"), None),
    )
    out_specs = P(("groups", "pages"), None)
    return jax.shard_map(body, mesh=mesh, in_specs=in_specs, out_specs=out_specs, check_vma=False)
```

profile of v0, /device:TPU:0, one launch (start us, length us, event | category | flops | bytes accessed | tf_op | source)
XLA Modules:
  0.0 81.3 jit_solution(7018582230763072979)
XLA Ops:
  0.0 0.0 copy-start
  0.0 0.7 compare_select_fusion.3
  0.7 0.1 reshape.214
  0.8 0.8 gather_fusion
  1.6 0.1 reshape.213
  1.7 0.7 compare_and_fusion
  2.4 0.1 div.46
  2.5 0.1 div.45
  2.6 0.1 broadcast_in_dim.39
  2.6 0.1 mul.17
  2.7 0.1 rem.60
  2.8 0.1 ne.103
  2.9 0.1 fusion.4
  3.0 0.1 reduce_window_sum.11
  3.1 0.2 select_reduce_fusion
  3.2 0.1 and.53
  3.3 0.6 broadcast_in_dim.36
  3.9 10.2 %scatter_fusion = s32[4,48]{1,0:T(4,128)} fusion(s32[4,48]{1,0:T(4,128)} %broadcast_in_dim.36, s32[64]{0:T(128)S(1)} %get-tuple-element.42, s32[64]{0:T(128)S(1)} %get-tuple-element.45), kind=kCustom, calls=%fused_computation.3 | custom fusion | bytes 1280 | tf_op jit(solution)/shard_map/scatter | solution.py:38
  14.1 6.3 %all-to-all-start = ((s32[4,1,48]{2,1,0:T(1,128)}), s32[4,1,48]{2,1,0:T(1,128)S(1)}, u32[]{:S(2)}, u32[]{:S(2)}) async-start(s32[4,1,48]{2,1,0:T(1,128)} %bitcast.6), calls=%async_computation | async-start | bytes 4096 | tf_op jit(solution)/shard_map/all_to_all | solution.py:57
  20.5 5.4 %all_gather.9 = bf16[2,32,128]{2,1,0:T(8,128)(2,1)S(1)} all-gather(bf16[2,8,128]{2,1,0:T(8,128)(2,1)} %param.6), channel_id=1, replica_groups=mesh['groups'=2,'pages'=4,'patches'=4] {'patches'}, dimensions={1}, use_global_device_ids=true | all-gather | bytes 20480 | tf_op jit(solution)/shard_map/all_gather | solution.py:48
  25.9 13.7 %all_gather.10 = bf16[8,32,128]{2,1,0:T(8,128)(2,1)S(1)} all-gather(bf16[2,32,128]{2,1,0:T(8,128)(2,1)S(1)} %all_gather.9), channel_id=1, replica_groups=mesh['groups'=2,'pages'=4,'patches'=4] {'pages'}, dimensions={0}, use_global_device_ids=true | all-gather | bytes 81920 | tf_op jit(solution)/shard_map/all_gather | solution.py:49
  39.5 15.2 %while.10 = (s32[]{:T(128)}, f32[10,8,256]{2,1,0:T(8,128)S(1)}, bf16[10,8,256,128]{3,2,1,0:T(8,128)(2,1)}, bf16[256,128]{1,0:T(8,128)(2,1)S(1)}, s32[]{:T(128)}) while((s32[]{:T(128)}, f32[10,8,256]{2,1,0:T(8,128)S(1)}, bf16[10,8,256,128]{3,2,1,0:T(8,128)(2,1)}, bf16[256,128]{1,0:T(8,128)(2,1)S(1)}, s32[]{:T(128)}) %tuple.28), condition=%wide.region_5.6_spmd, body=%wide.region_3.5_spmd.sunk | while | flops 134739968 | bytes 614477 | solution.py:18
  39.5 1.5 %convolution_reduce_fusion.2 = f32[8,256]{1,0:T(8,128)S(1)} fusion(bf16[10,8,256,128]{3,2,1,0:T(8,128)(2,1)} %get-tuple-element.84, s32[]{:T(128)S(6)} %copy.20, bf16[256,128]{1,0:T(8,128)(2,1)S(1)} %get-tuple-element.85), kind=kOutput, calls=%fused_computation.4.clone.1 | convolution fusion | flops 134739968 | bytes 598020 | tf_op jit(solution)/shard_map/while/body/eval_jaxpr/rd,bpd->brp/dot_general | solution.py:15
  41.1 1.5 %convolution_reduce_fusion.2 = f32[8,256]{1,0:T(8,128)S(1)} fusion(bf16[10,8,256,128]{3,2,1,0:T(8,128)(2,1)} %get-tuple-element.84, s32[]{:T(128)S(6)} %copy.20, bf16[256,128]{1,0:T(8,128)(2,1)S(1)} %get-tuple-element.85), kind=kOutput, calls=%fused_computation.4.clone.1 | convolution fusion | flops 134739968 | bytes 598020 | tf_op jit(solution)/shard_map/while/body/eval_jaxpr/rd,bpd->brp/dot_general | solution.py:15
  42.6 1.5 %convolution_reduce_fusion.2 = f32[8,256]{1,0:T(8,128)S(1)} fusion(bf16[10,8,256,128]{3,2,1,0:T(8,128)(2,1)} %get-tuple-element.84, s32[]{:T(128)S(6)} %copy.20, bf16[256,128]{1,0:T(8,128)(2,1)S(1)} %get-tuple-element.85), kind=kOutput, calls=%fused_computation.4.clone.1 | convolution fusion | flops 134739968 | bytes 598020 | tf_op jit(solution)/shard_map/while/body/eval_jaxpr/rd,bpd->brp/dot_general | solution.py:15
  44.1 1.5 %convolution_reduce_fusion.2 = f32[8,256]{1,0:T(8,128)S(1)} fusion(bf16[10,8,256,128]{3,2,1,0:T(8,128)(2,1)} %get-tuple-element.84, s32[]{:T(128)S(6)} %copy.20, bf16[256,128]{1,0:T(8,128)(2,1)S(1)} %get-tuple-element.85), kind=kOutput, calls=%fused_computation.4.clone.1 | convolution fusion | flops 134739968 | bytes 598020 | tf_op jit(solution)/shard_map/while/body/eval_jaxpr/rd,bpd->brp/dot_general | solution.py:15
  45.6 1.5 %convolution_reduce_fusion.2 = f32[8,256]{1,0:T(8,128)S(1)} fusion(bf16[10,8,256,128]{3,2,1,0:T(8,128)(2,1)} %get-tuple-element.84, s32[]{:T(128)S(6)} %copy.20, bf16[256,128]{1,0:T(8,128)(2,1)S(1)} %get-tuple-element.85), kind=kOutput, calls=%fused_computation.4.clone.1 | convolution fusion | flops 134739968 | bytes 598020 | tf_op jit(solution)/shard_map/while/body/eval_jaxpr/rd,bpd->brp/dot_general | solution.py:15
  47.2 1.5 %convolution_reduce_fusion.2 = f32[8,256]{1,0:T(8,128)S(1)} fusion(bf16[10,8,256,128]{3,2,1,0:T(8,128)(2,1)} %get-tuple-element.84, s32[]{:T(128)S(6)} %copy.20, bf16[256,128]{1,0:T(8,128)(2,1)S(1)} %get-tuple-element.85), kind=kOutput, calls=%fused_computation.4.clone.1 | convolution fusion | flops 134739968 | bytes 598020 | tf_op jit(solution)/shard_map/while/body/eval_jaxpr/rd,bpd->brp/dot_general | solution.py:15
  48.7 1.5 %convolution_reduce_fusion.2 = f32[8,256]{1,0:T(8,128)S(1)} fusion(bf16[10,8,256,128]{3,2,1,0:T(8,128)(2,1)} %get-tuple-element.84, s32[]{:T(128)S(6)} %copy.20, bf16[256,128]{1,0:T(8,128)(2,1)S(1)} %get-tuple-element.85), kind=kOutput, calls=%fused_computation.4.clone.1 | convolution fusion | flops 134739968 | bytes 598020 | tf_op jit(solution)/shard_map/while/body/eval_jaxpr/rd,bpd->brp/dot_general | solution.py:15
  50.2 1.5 %convolution_reduce_fusion.2 = f32[8,256]{1,0:T(8,128)S(1)} fusion(bf16[10,8,256,128]{3,2,1,0:T(8,128)(2,1)} %get-tuple-element.84, s32[]{:T(128)S(6)} %copy.20, bf16[256,128]{1,0:T(8,128)(2,1)S(1)} %get-tuple-element.85), kind=kOutput, calls=%fused_computation.4.clone.1 | convolution fusion | flops 134739968 | bytes 598020 | tf_op jit(solution)/shard_map/while/body/eval_jaxpr/rd,bpd->brp/dot_general | solution.py:15
  51.7 1.5 %convolution_reduce_fusion.2 = f32[8,256]{1,0:T(8,128)S(1)} fusion(bf16[10,8,256,128]{3,2,1,0:T(8,128)(2,1)} %get-tuple-element.84, s32[]{:T(128)S(6)} %copy.20, bf16[256,128]{1,0:T(8,128)(2,1)S(1)} %get-tuple-element.85), kind=kOutput, calls=%fused_computation.4.clone.1 | convolution fusion | flops 134739968 | bytes 598020 | tf_op jit(solution)/shard_map/while/body/eval_jaxpr/rd,bpd->brp/dot_general | solution.py:15
  53.3 1.5 %convolution_reduce_fusion.2 = f32[8,256]{1,0:T(8,128)S(1)} fusion(bf16[10,8,256,128]{3,2,1,0:T(8,128)(2,1)} %get-tuple-element.84, s32[]{:T(128)S(6)} %copy.20, bf16[256,128]{1,0:T(8,128)(2,1)S(1)} %get-tuple-element.85), kind=kOutput, calls=%fused_computation.4.clone.1 | convolution fusion | flops 134739968 | bytes 598020 | tf_op jit(solution)/shard_map/while/body/eval_jaxpr/rd,bpd->brp/dot_general | solution.py:15
  54.8 0.6 all_to_all.20
  55.4 0.0 all-to-all-done
  55.4 3.3 %all-to-all-start.1 = ((f32[4,20,256]{2,1,0:T(8,128)}), f32[4,20,256]{2,1,0:T(8,128)S(1)}, u32[]{:S(2)}, u32[]{:S(2)}) async-start(f32[4,20,256]{2,1,0:T(8,128)} %all_to_all.20), calls=%async_computation.1 | async-start | bytes 196608 | tf_op jit(solution)/shard_map/all_to_all | solution.py:52
  58.7 0.2 broadcast_maximum_fusion
  59.0 0.1 reshape.220
  59.1 3.9 %all-to-all-done.1 = f32[4,20,256]{2,1,0:T(8,128)S(1)} async-done(((f32[4,20,256]{2,1,0:T(8,128)}), f32[4,20,256]{2,1,0:T(8,128)S(1)}, u32[]{:S(2)}, u32[]{:S(2)}) %all-to-all-start.1) | async-done | bytes 81952 | tf_op jit(solution)/shard_map/all_to_all | solution.py:52
  63.0 0.1 reshape.210
  63.1 0.1 reduce_sum.22
  63.2 0.1 copy.12
  63.3 5.2 %all-gather = f32[4,20,8]{1,2,0:T(8,128)S(1)} all-gather(f32[1,20,8]{1,2,0:T(8,128)S(1)} %copy.12), channel_id=1, replica_groups=mesh['groups'=2,'pages'=4,'patches'=4] {'patches'}, dimensions={0}, use_global_device_ids=true | all-gather | bytes 3200 | tf_op jit(solution)/shard_map/all_gather | solution.py:55
  68.5 0.1 reshape.242
  68.6 1.2 %gather_fusion.1 = f32[192]{0:T(256)S(1)} fusion(f32[80,8]{0,1:T(8,128)S(1)} %reshape.242, s32[192]{0:T(256)S(1)} %reshape.220), kind=kCustom, calls=%fused_computation.1 | custom fusion | bytes 3072 | tf_op jit(solution)/shard_map/gather | solution.py:59
  69.7 0.1 gather.14
  69.8 9.9 %all_to_all.27 = f32[4,1,48]{2,1,0:T(1,128)S(1)} all-to-all(f32[4,1,48]{2,1,0:T(1,128)S(1)} %compare_select_fusion), channel_id=1, replica_groups=mesh['groups'=2,'pages'=4,'patches'=4] {'pages'}, dimensions={0} | all-to-all | bytes 1536 | tf_op jit(solution)/shard_map/all_to_all | solution.py:61
  79.7 0.9 %gather_fusion.2 = f32[64]{0:T(128)S(1)} fusion(f32[4,48]{1,0:T(4,128)S(1)} %bitcast.60, s32[64]{0:T(128)S(1)} %get-tuple-element.41), kind=kCustom, calls=%fused_computation.2 | custom fusion | bytes 1024 | tf_op jit(solution)/shard_map/gather | solution.py:62
  80.6 0.6 reshape.211
  (23 shorter events, 0.2 us)
Async XLA Ops:
  0.0 0.8 copy-start
  14.1 41.3 %all-to-all-start = ((s32[4,1,48]{2,1,0:T(1,128)}), s32[4,1,48]{2,1,0:T(1,128)S(1)}, u32[]{:S(2)}, u32[]{:S(2)}) async-start(s32[4,1,48]{2,1,0:T(1,128)} %bitcast.6), calls=%async_computation | async-start | bytes 4096 | tf_op jit(solution)/shard_map/all_to_all | solution.py:57
  55.4 7.6 %all-to-all-start.1 = ((f32[4,20,256]{2,1,0:T(8,128)}), f32[4,20,256]{2,1,0:T(8,128)S(1)}, u32[]{:S(2)}, u32[]{:S(2)}) async-start(f32[4,20,256]{2,1,0:T(8,128)} %all_to_all.20), calls=%async_computation.1 | async-start | bytes 196608 | tf_op jit(solution)/shard_map/all_to_all | solution.py:52
where the time goes:
time: 82.3 us; the launch traced here: 81.3 us
  blocking collectives  34.2 us (42%)
  local copies, waits for them, and re-layouts  16.2 us (20%)
  matrix products  14.9 us (18%)
  starting transfers between devices  9.65 us (12%)
  waiting for transfers between devices  3.93 us (5%)
  other arithmetic  2.15 us (3%)
    dot_general x10, matrix products, per_block(): jnp.einsum('rd,bpd->brp', query_rows, block, preferred_element_type=jnp.f...  14.9 us
    all_gather x1, blocking collectives, body(): shard_rows = lax.all_gather(local_tokens, 'pages', axis=0, tiled=True)  13.7 us
    scatter x1, local copies, waits for them, and re-layouts, slot_plan(): codes = jnp.full((owner_count, CAP), -1, jnp.int32).at[holder, rank].set(...  10.2 us
    all_to_all x1, blocking collectives, body(): lax.all_to_all(picked, 'pages', split_axis=0, concat_axis=0, tiled=True)  9.92 us
    all_to_all x1, starting transfers between devices, body(): lax.all_to_all(codes, 'pages', split_axis=0, concat_axis=0, tiled=True)  6.35 us
    all_gather x1, blocking collectives, body(): local_tokens = lax.all_gather(queries, 'patches', axis=1, tiled=True)  5.37 us
    all_gather x1, blocking collectives, body(): page_scores = lax.all_gather(share_scores, 'patches', axis=0, tiled=True)  5.19 us
    all_to_all x1, waiting for transfers between devices, body(): lax.all_to_all(maxima, 'patches', split_axis=0, concat_axis=0, tiled=True)  3.93 us
  transfers between devices with their start and end apart: 2, of which 1 were waited for; matrix products, arithmetic and copies ran while one was open for 19% of the time, Pallas kernels for 0%

commit v1 on v0

--- a/solution.py
+++ b/solution.py
@@ -52,7 +52,14 @@
     arrived = lax.all_to_all(maxima, "patches", split_axis=0, concat_axis=0, tiled=True)
     share_max = jnp.max(arrived.reshape(part_count, page_count // part_count, -1), axis=0)
     share_scores = jnp.mean(share_max.reshape(page_count // part_count, -1, QT), axis=2)
-    page_scores = lax.all_gather(share_scores, "patches", axis=0, tiled=True)
+    ring = [share_scores]
+    for hop in range(3):
+        ring.append(lax.ppermute(ring[-1], "patches", [(dev, (dev + 1) % 4) for dev in range(4)]))
+    page_scores = jnp.roll(
+        jnp.concatenate(ring[::-1], axis=0),
+        (lax.axis_index("patches") + 1) * ring[0].shape[0],
+        axis=0,
+    )
     holder, rank, codes = slot_plan(storage, page_count, owner_count, query_count)
     incoming = lax.all_to_all(codes, "pages", split_axis=0, concat_axis=0, tiled=True)
     safe_codes = jnp.maximum(incoming, 0)

time: 82.3 us -> 82.5 us (level)
  waiting for transfers between devices: 3.93 us -> 8.85 us
  blocking collectives: 34.2 us -> 30.8 us
  starting transfers between devices: 9.65 us -> 8.22 us
    ppermute x0 -> x3, waiting for transfers between devices: none -> 6.66 us  [body(): lax.ppermute(ring[-1], 'patches', [(dev, (dev + 1) % 4) for dev in range(...]
    all_gather x1 -> x0, blocking collectives: 5.19 us -> none  [body(): page_scores = lax.all_gather(share_scores, 'patches', axis=0, tiled=True)]
    all_to_all x1, waiting for transfers between devices: 3.93 us -> 0.01 us  [body(): lax.all_to_all(maxima, 'patches', split_axis=0, concat_axis=0, tiled=True)]
    all_to_all x1, waiting for transfers between devices: 0.01 us -> 2.19 us  [body(): lax.all_to_all(codes, 'pages', split_axis=0, concat_axis=0, tiled=True)]
    all_to_all x1, starting transfers between devices: 6.35 us -> 4.68 us  [body(): lax.all_to_all(codes, 'pages', split_axis=0, concat_axis=0, tiled=True)]
    all_gather x1, blocking collectives: 5.37 us -> 6.53 us  [body(): local_tokens = lax.all_gather(queries, 'patches', axis=1, tiled=True)]
  transfers between devices with their start and end apart: 2 -> 5, of which waited for: 1 -> 4; matrix products, arithmetic and copies ran while one was open for 19% -> 17% of each run, Pallas kernels for 0% -> 0%
where the time goes in v1:
time: 82.5 us; the launch traced here: 81.5 us
  blocking collectives  30.8 us (37%)
  local copies, waits for them, and re-layouts  16.9 us (20%)
  matrix products  14.8 us (18%)
  waiting for transfers between devices  8.85 us (11%)
  starting transfers between devices  8.22 us (10%)
  other arithmetic  1.45 us (2%)
    dot_general x10, matrix products, per_block(): jnp.einsum('rd,bpd->brp', query_rows, block, preferred_element_type=jnp.f...  14.8 us
    all_gather x1, blocking collectives, body(): shard_rows = lax.all_gather(local_tokens, 'pages', axis=0, tiled=True)  13.8 us
    all_to_all x1, blocking collectives, body(): lax.all_to_all(picked, 'pages', split_axis=0, concat_axis=0, tiled=True)  10.5 us
    scatter x1, local copies, waits for them, and re-layouts, slot_plan(): codes = jnp.full((owner_count, CAP), -1, jnp.int32).at[holder, rank].set(...  10.2 us
    ppermute x3, waiting for transfers between devices, body(): lax.ppermute(ring[-1], 'patches', [(dev, (dev + 1) % 4) for dev in range(...  6.66 us
    all_gather x1, blocking collectives, body(): local_tokens = lax.all_gather(queries, 'patches', axis=1, tiled=True)  6.53 us
    all_to_all x1, starting transfers between devices, body(): lax.all_to_all(codes, 'pages', split_axis=0, concat_axis=0, tiled=True)  4.68 us
    all_to_all x1, starting transfers between devices, body(): lax.all_to_all(maxima, 'patches', split_axis=0, concat_axis=0, tiled=True)  3.3 us
  transfers between devices with their start and end apart: 5, of which 4 were waited for; matrix products, arithmetic and copies ran while one was open for 17% of the time, Pallas kernels for 0%

profile of v1, /device:TPU:0, one launch (start us, length us, event | category | flops | bytes accessed | tf_op | source)
XLA Modules:
  0.0 81.5 jit_solution(5500126743248588635)
XLA Ops:
  0.0 6.5 %all_gather.6 = bf16[2,32,128]{2,1,0:T(8,128)(2,1)S(1)} all-gather(bf16[2,8,128]{2,1,0:T(8,128)(2,1)} %param.6), channel_id=1, replica_groups=mesh['groups'=2,'pages'=4,'patches'=4] {'patches'}, dimensions={1}, use_global_device_ids=true | all-gather | bytes 20480 | tf_op jit(solution)/shard_map/all_gather | solution.py:48
  6.5 13.8 %all_gather.7 = bf16[8,32,128]{2,1,0:T(8,128)(2,1)S(1)} all-gather(bf16[2,32,128]{2,1,0:T(8,128)(2,1)S(1)} %all_gather.6), channel_id=1, replica_groups=mesh['groups'=2,'pages'=4,'patches'=4] {'pages'}, dimensions={0}, use_global_device_ids=true | all-gather | bytes 81920 | tf_op jit(solution)/shard_map/all_gather | solution.py:49
  20.3 15.2 %while.10 = (s32[]{:T(128)}, f32[10,8,256]{2,1,0:T(8,128)S(1)}, bf16[10,8,256,128]{3,2,1,0:T(8,128)(2,1)}, bf16[256,128]{1,0:T(8,128)(2,1)S(1)}, s32[]{:T(128)}) while((s32[]{:T(128)}, f32[10,8,256]{2,1,0:T(8,128)S(1)}, bf16[10,8,256,128]{3,2,1,0:T(8,128)(2,1)}, bf16[256,128]{1,0:T(8,128)(2,1)S(1)}, s32[]{:T(128)}) %tuple.28), condition=%wide.region_5.6_spmd, body=%wide.region_3.5_spmd.sunk | while | flops 134739968 | bytes 614477 | solution.py:18
  20.3 1.5 %convolution_reduce_fusion.2 = f32[8,256]{1,0:T(8,128)S(1)} fusion(bf16[10,8,256,128]{3,2,1,0:T(8,128)(2,1)} %get-tuple-element.84, s32[]{:T(128)S(6)} %copy.30, bf16[256,128]{1,0:T(8,128)(2,1)S(1)} %get-tuple-element.85), kind=kOutput, calls=%fused_computation.4.clone.1 | convolution fusion | flops 134739968 | bytes 598020 | tf_op jit(solution)/shard_map/while/body/eval_jaxpr/rd,bpd->brp/dot_general | solution.py:15
  21.9 1.5 %convolution_reduce_fusion.2 = f32[8,256]{1,0:T(8,128)S(1)} fusion(bf16[10,8,256,128]{3,2,1,0:T(8,128)(2,1)} %get-tuple-element.84, s32[]{:T(128)S(6)} %copy.30, bf16[256,128]{1,0:T(8,128)(2,1)S(1)} %get-tuple-element.85), kind=kOutput, calls=%fused_computation.4.clone.1 | convolution fusion | flops 134739968 | bytes 598020 | tf_op jit(solution)/shard_map/while/body/eval_jaxpr/rd,bpd->brp/dot_general | solution.py:15
  23.4 1.5 %convolution_reduce_fusion.2 = f32[8,256]{1,0:T(8,128)S(1)} fusion(bf16[10,8,256,128]{3,2,1,0:T(8,128)(2,1)} %get-tuple-element.84, s32[]{:T(128)S(6)} %copy.30, bf16[256,128]{1,0:T(8,128)(2,1)S(1)} %get-tuple-element.85), kind=kOutput, calls=%fused_computation.4.clone.1 | convolution fusion | flops 134739968 | bytes 598020 | tf_op jit(solution)/shard_map/while/body/eval_jaxpr/rd,bpd->brp/dot_general | solution.py:15
  24.9 1.5 %convolution_reduce_fusion.2 = f32[8,256]{1,0:T(8,128)S(1)} fusion(bf16[10,8,256,128]{3,2,1,0:T(8,128)(2,1)} %get-tuple-element.84, s32[]{:T(128)S(6)} %copy.30, bf16[256,128]{1,0:T(8,128)(2,1)S(1)} %get-tuple-element.85), kind=kOutput, calls=%fused_computation.4.clone.1 | convolution fusion | flops 134739968 | bytes 598020 | tf_op jit(solution)/shard_map/while/body/eval_jaxpr/rd,bpd->brp/dot_general | solution.py:15
  26.4 1.5 %convolution_reduce_fusion.2 = f32[8,256]{1,0:T(8,128)S(1)} fusion(bf16[10,8,256,128]{3,2,1,0:T(8,128)(2,1)} %get-tuple-element.84, s32[]{:T(128)S(6)} %copy.30, bf16[256,128]{1,0:T(8,128)(2,1)S(1)} %get-tuple-element.85), kind=kOutput, calls=%fused_computation.4.clone.1 | convolution fusion | flops 134739968 | bytes 598020 | tf_op jit(solution)/shard_map/while/body/eval_jaxpr/rd,bpd->brp/dot_general | solution.py:15
  27.9 1.5 %convolution_reduce_fusion.2 = f32[8,256]{1,0:T(8,128)S(1)} fusion(bf16[10,8,256,128]{3,2,1,0:T(8,128)(2,1)} %get-tuple-element.84, s32[]{:T(128)S(6)} %copy.30, bf16[256,128]{1,0:T(8,128)(2,1)S(1)} %get-tuple-element.85), kind=kOutput, calls=%fused_computation.4.clone.1 | convolution fusion | flops 134739968 | bytes 598020 | tf_op jit(solution)/shard_map/while/body/eval_jaxpr/rd,bpd->brp/dot_general | solution.py:15
  29.5 1.5 %convolution_reduce_fusion.2 = f32[8,256]{1,0:T(8,128)S(1)} fusion(bf16[10,8,256,128]{3,2,1,0:T(8,128)(2,1)} %get-tuple-element.84, s32[]{:T(128)S(6)} %copy.30, bf16[256,128]{1,0:T(8,128)(2,1)S(1)} %get-tuple-element.85), kind=kOutput, calls=%fused_computation.4.clone.1 | convolution fusion | flops 134739968 | bytes 598020 | tf_op jit(solution)/shard_map/while/body/eval_jaxpr/rd,bpd->brp/dot_general | solution.py:15
  31.0 1.5 %convolution_reduce_fusion.2 = f32[8,256]{1,0:T(8,128)S(1)} fusion(bf16[10,8,256,128]{3,2,1,0:T(8,128)(2,1)} %get-tuple-element.84, s32[]{:T(128)S(6)} %copy.30, bf16[256,128]{1,0:T(8,128)(2,1)S(1)} %get-tuple-element.85), kind=kOutput, calls=%fused_computation.4.clone.1 | convolution fusion | flops 134739968 | bytes 598020 | tf_op jit(solution)/shard_map/while/body/eval_jaxpr/rd,bpd->brp/dot_general | solution.py:15
  32.5 1.5 %convolution_reduce_fusion.2 = f32[8,256]{1,0:T(8,128)S(1)} fusion(bf16[10,8,256,128]{3,2,1,0:T(8,128)(2,1)} %get-tuple-element.84, s32[]{:T(128)S(6)} %copy.30, bf16[256,128]{1,0:T(8,128)(2,1)S(1)} %get-tuple-element.85), kind=kOutput, calls=%fused_computation.4.clone.1 | convolution fusion | flops 134739968 | bytes 598020 | tf_op jit(solution)/shard_map/while/body/eval_jaxpr/rd,bpd->brp/dot_general | solution.py:15
  34.0 1.5 %convolution_reduce_fusion.2 = f32[8,256]{1,0:T(8,128)S(1)} fusion(bf16[10,8,256,128]{3,2,1,0:T(8,128)(2,1)} %get-tuple-element.84, s32[]{:T(128)S(6)} %copy.30, bf16[256,128]{1,0:T(8,128)(2,1)S(1)} %get-tuple-element.85), kind=kOutput, calls=%fused_computation.4.clone.1 | convolution fusion | flops 134739968 | bytes 598020 | tf_op jit(solution)/shard_map/while/body/eval_jaxpr/rd,bpd->brp/dot_general | solution.py:15
  35.5 0.6 all_to_all.20
  36.2 3.3 %all-to-all-start.1 = ((f32[4,20,256]{2,1,0:T(8,128)}), f32[4,20,256]{2,1,0:T(8,128)S(1)}, u32[]{:S(2)}, u32[]{:S(2)}) async-start(f32[4,20,256]{2,1,0:T(8,128)} %all_to_all.20), calls=%async_computation.1 | async-start | bytes 196608 | tf_op jit(solution)/shard_map/all_to_all | solution.py:52
  39.5 0.7 compare_select_fusion.3
  40.2 0.1 reshape.214
  40.3 0.8 gather_fusion
  41.1 0.1 reshape.213
  41.2 0.1 div.46
  41.3 0.1 div.45
  41.4 0.1 broadcast_in_dim.39
  41.4 0.1 mul.20
  41.5 0.1 rem.65
  41.6 0.1 ne.111
  41.7 0.1 fusion.4
  41.8 0.1 reduce_window_sum.11
  41.9 0.2 select_reduce_fusion
  42.0 0.1 and.59
  42.2 0.6 broadcast_in_dim.36
  42.8 10.2 %scatter_fusion = s32[4,48]{1,0:T(4,128)} fusion(s32[4,48]{1,0:T(4,128)} %broadcast_in_dim.36, s32[64]{0:T(128)S(1)} %get-tuple-element.42, s32[64]{0:T(128)S(1)} %get-tuple-element.45), kind=kCustom, calls=%fused_computation.3 | custom fusion | bytes 1280 | tf_op jit(solution)/shard_map/scatter | solution.py:38
  53.0 0.0 all-to-all-done.1
  53.0 4.7 %all-to-all-start = ((s32[4,1,48]{2,1,0:T(1,128)}), s32[4,1,48]{2,1,0:T(1,128)S(1)}, u32[]{:S(2)}, u32[]{:S(2)}) async-start(s32[4,1,48]{2,1,0:T(1,128)} %bitcast.6), calls=%async_computation | async-start | bytes 4096 | tf_op jit(solution)/shard_map/all_to_all | solution.py:64
  57.7 0.1 reshape.210
  57.7 0.1 reduce_sum.22
  57.9 0.2 collective-permute-start
  58.1 2.9 %collective-permute-done = f32[20,8]{1,0:T(8,128)S(1)} collective-permute-done((f32[20,8]{1,0:T(8,128)S(1)}, f32[20,8]{1,0:T(8,128)S(1)}, u32[]{:S(2)}, u32[]{:S(2)}) %collective-permute-start) | collective-permute-done | bytes 672 | tf_op jit(solution)/shard_map/ppermute | solution.py:57
  61.0 2.2 %all-to-all-done = s32[4,1,48]{2,1,0:T(1,128)S(1)} async-done(((s32[4,1,48]{2,1,0:T(1,128)}), s32[4,1,48]{2,1,0:T(1,128)S(1)}, u32[]{:S(2)}, u32[]{:S(2)}) %all-to-all-start) | async-done | bytes 800 | tf_op jit(solution)/shard_map/all_to_all | solution.py:64
  63.2 0.2 broadcast_maximum_fusion
  63.4 0.7 collective-permute-done.1
  64.2 0.1 reshape.220
  64.3 3.0 %collective-permute-done.2 = f32[20,8]{1,0:T(8,128)S(1)} collective-permute-done((f32[20,8]{1,0:T(8,128)S(1)}, f32[20,8]{1,0:T(8,128)S(1)}, u32[]{:S(2)}, u32[]{:S(2)}) %collective-permute-start.2) | collective-permute-done | bytes 672 | tf_op jit(solution)/shard_map/ppermute | solution.py:57
  67.3 0.5 concatenate.14
  67.8 1.6 %gather_fusion.1 = f32[192]{0:T(256)S(1)} fusion(f32[80,8]{1,0:T(8,128)S(1)} %constant_dynamic-slice_fusion, s32[192]{0:T(256)S(1)} %reshape.220), kind=kCustom, calls=%fused_computation.1 | custom fusion | bytes 3072 | tf_op jit(solution)/shard_map/gather | solution.py:66
  69.4 0.1 gather.14
  69.5 10.5 %all_to_all.27 = f32[4,1,48]{2,1,0:T(1,128)S(1)} all-to-all(f32[4,1,48]{2,1,0:T(1,128)S(1)} %compare_select_fusion), channel_id=1, replica_groups=mesh['groups'=2,'pages'=4,'patches'=4] {'pages'}, dimensions={0} | all-to-all | bytes 1536 | tf_op jit(solution)/shard_map/all_to_all | solution.py:68
  80.0 0.9 %gather_fusion.2 = f32[64]{0:T(128)S(1)} fusion(f32[4,48]{1,0:T(4,128)S(1)} %bitcast.56, s32[64]{0:T(128)S(1)} %get-tuple-element.41), kind=kCustom, calls=%fused_computation.2 | custom fusion | bytes 1024 | tf_op jit(solution)/shard_map/gather | solution.py:69
  80.8 0.6 reshape.211
  (29 shorter events, 0.2 us)
Async XLA Ops:
  0.0 40.3 %copy-start = (s32[320]{0:T(512)S(1)}, s32[320]{0:T(512)}, u32[]{:S(2)}) copy-start(s32[320]{0:T(512)} %param.8) | copy-start | bytes 3844
  0.0 41.2 %copy-start.1 = (s32[2,32]{1,0:T(2,128)S(1)}, s32[2,32]{1,0:T(2,128)}, u32[]{:S(2)}) copy-start(s32[2,32]{1,0:T(2,128)} %param.9) | copy-start | bytes 772
  36.2 16.8 %all-to-all-start.1 = ((f32[4,20,256]{2,1,0:T(8,128)}), f32[4,20,256]{2,1,0:T(8,128)S(1)}, u32[]{:S(2)}, u32[]{:S(2)}) async-start(f32[4,20,256]{2,1,0:T(8,128)} %all_to_all.20), calls=%async_computation.1 | async-start | bytes 196608 | tf_op jit(solution)/shard_map/all_to_all | solution.py:52
  53.0 10.3 %all-to-all-start = ((s32[4,1,48]{2,1,0:T(1,128)}), s32[4,1,48]{2,1,0:T(1,128)S(1)}, u32[]{:S(2)}, u32[]{:S(2)}) async-start(s32[4,1,48]{2,1,0:T(1,128)} %bitcast.6), calls=%async_computation | async-start | bytes 4096 | tf_op jit(solution)/shard_map/all_to_all | solution.py:64
  57.9 3.2 %collective-permute-start = (f32[20,8]{1,0:T(8,128)S(1)}, f32[20,8]{1,0:T(8,128)S(1)}, u32[]{:S(2)}, u32[]{:S(2)}) collective-permute-start(f32[20,8]{1,0:T(8,128)S(1)} %broadcast_multiply_fusion), channel_id=1, source_target_pairs={{0,1},{1,2},{2,3},{3,0},{4,5},{5,6},{6,7},{7,4},{8,9},{9,10},{10,1... | collective-permute-start | bytes 1928 | tf_op jit(solution)/shard_map/ppermute | solution.py:57
  61.0 3.1 %collective-permute-start.1 = (f32[20,8]{1,0:T(8,128)S(1)}, f32[20,8]{1,0:T(8,128)S(1)}, u32[]{:S(2)}, u32[]{:S(2)}) collective-permute-start(f32[20,8]{1,0:T(8,128)S(1)} %collective-permute-done), channel_id=1, source_target_pairs={{0,1},{1,2},{2,3},{3,0},{4,5},{5,6},{6,7},{7,4},{8,9},{9,10},{10,1... | collective-permute-start | bytes 1928 | tf_op jit(solution)/shard_map/ppermute | solution.py:57
  64.1 3.1 %collective-permute-start.2 = (f32[20,8]{1,0:T(8,128)S(1)}, f32[20,8]{1,0:T(8,128)S(1)}, u32[]{:S(2)}, u32[]{:S(2)}) collective-permute-start(f32[20,8]{1,0:T(8,128)S(1)} %collective-permute-done.1), channel_id=1, source_target_pairs={{0,1},{1,2},{2,3},{3,0},{4,5},{5,6},{6,7},{7,4},{8,9},{9,10},{10,1... | collective-permute-start | bytes 1928 | tf_op jit(solution)/shard_map/ppermute | solution.py:57
